TPU v7x, 32 devices: a whole 2x2x4 slice. The times are simulated.
32 devices in a mesh: section: 4 (over z), col: 8 (over y, x, core).
Axes of the slice: x: 2, y: 2, z: 4, core: 2. Of those that a mesh axis runs over, the one named last changes fastest.
Arguments:
- tiles: bfloat16 [256, 12, 128, 128], P('col', None, 'section'), may hold values from 0.0099487305 to 1
- offsets: int32 [256, 12], replicated, may hold values from -6 to 6, as said below
- counts: int32 [256], replicated, may hold values from 1 to 12
- ranks: int32 [256, 25, 128, 128], P('col', None, 'section'), may hold values from 0 to 3199, as said below
Outputs:
- pruned: bfloat16 [256, 25, 128, 128], P('col', None, 'section')
Inputs may be any that keep to these rules, and one draw needn't show every extreme that they name: Within each panel the 12 offsets are distinct, each from -6 to 6. For every panel j and column c, ranks[j, :, c, :] holds each of 0 .. 3199 once.
All inputs are finite; a program needn't handle non-finite values.
Results may differ from a plain program's by a relative error of at most 0.001.
Values may be sent and summed in bfloat16 or wider, within the bound.
A program may use at most 128 MiB of HBM per device.

v0:
```python
import jax
import jax.numpy as jnp
from jax import lax
from jax.sharding import PartitionSpec as P

W = 6
TOPK = 256


def extended(shard, sides, width):
    for axis, dim in sides:
        count, length = (lax.axis_size(axis), shard.shape[dim])
        up = [(i, (i + 1) % count) for i in range(count - 1)]
        down = [(j, i) for i, j in up]
        last = lax.slice_in_dim(shard, length - width, length, axis=dim)
        initial = lax.slice_in_dim(shard, 0, width, axis=dim)
        before = lax.ppermute(last, axis, up)
        after = lax.ppermute(initial, axis, down)
        shard = jnp.concatenate([before, shard, after], axis=dim)
    return shard


def expand(own, own_off, own_cnt, center, global_panel, banded, band_off, band_cnt, total, bands):
    slots = own.shape[0]
    slot_ids = jnp.arange(slots, dtype=jnp.int32)
    where_at = center + W + own_off
    firsts = banded[where_at]
    first_off = band_off[where_at]
    first_cnt = band_cnt[where_at]
    row_own = global_panel + own_off
    ok_own = (slot_ids < own_cnt) & (row_own >= 0) & (row_own < total)
    row_first = row_own[:, None] + first_off
    ok_first = (slot_ids[None, :] < first_cnt[:, None]) & (row_first >= 0) & (row_first < total)
    weight = (ok_own[:, None] & ok_first).astype(jnp.float32)
    target = own_off[:, None] + first_off + 2 * W
    products = jnp.einsum("kcx,klxr->klcr", own, firsts, preferred_element_type=jnp.float32)
    weighted = products * weight[:, :, None, None]
    columns = own.shape[1]
    rows = own.shape[2]
    empty = jnp.zeros((bands, columns, rows), jnp.float32)
    return empty.at[target.reshape(-1)].add(weighted.reshape((slots * slots, columns, rows)))


def finish(expanded, rank_block):
    keep = rank_block < TOPK
    squared = jnp.where(keep, expanded * expanded, jnp.float32(0.0))
    totals = jnp.sum(squared, axis=(0, 2), keepdims=True)
    return (TOPK * squared / (totals + 1e-06)).astype(jnp.bfloat16)


def shards(tiles, offsets, counts, ranks):
    panels = tiles.shape[0]
    slots = tiles.shape[1]
    bands = ranks.shape[1]
    total = offsets.shape[0]
    first_panel = lax.axis_index("col") * panels
    pad_off = jnp.concatenate(
        [jnp.zeros((W, slots), jnp.int32), offsets, jnp.zeros((W, slots), jnp.int32)], axis=0
    )
    pad_cnt = jnp.concatenate(
        [jnp.zeros((W,), jnp.int32), counts, jnp.zeros((W,), jnp.int32)], axis=0
    )
    whole_cols = lax.all_gather(tiles, "section", axis=2, tiled=True)
    banded = extended(whole_cols, (("col", 0),), W)
    band_off = lax.dynamic_slice_in_dim(pad_off, first_panel, panels + 2 * W, 0)
    band_cnt = lax.dynamic_slice_in_dim(pad_cnt, first_panel, panels + 2 * W, 0)
    own_off = lax.dynamic_slice_in_dim(offsets, first_panel, panels, 0)
    own_cnt = lax.dynamic_slice_in_dim(counts, first_panel, panels, 0)

    def one_panel(packed):
        own, p_off, p_cnt, rank_block, centre = packed
        values = expand(
            own,
            p_off,
            p_cnt,
            centre,
            first_panel + centre,
            banded,
            band_off,
            band_cnt,
            total,
            bands,
        )
        return finish(values, rank_block)

    return lax.map(one_panel, (tiles, own_off, own_cnt, ranks, jnp.arange(panels, dtype=jnp.int32)))


def solution(mesh):
    placed = (P("col", None, "section", None), P(), P(), P("col", None, "section", None))
    return jax.shard_map(
        shards,
        mesh=mesh,
        in_specs=placed,
        out_specs=P("col", None, "section", None),
        check_vma=False,
    )
```

profile of v0, /device:TPU:1, one launch (start us, length us, event | category | flops | bytes accessed | tf_op | source)
XLA Modules:
  0.0 1164.7 jit_solution(17251108781027687092)
XLA Ops:
  7.3 222.1 %all-gather.2.cloned.1.call-done = bf16[32,12,128,128]{3,2,1,0:T(8,128)(2,1)} async-done(((bf16[32,12,32,128]{3,2,1,0:T(8,128)(2,1)}), bf16[32,12,128,128]{3,2,1,0:T(8,128)(2,1)}) %all-gather.2.cloned.1.call-update) | async-done | bytes 12582928 | tf_op jit(solution)/shard_map/all_gather | solution.py:63
  241.7 23.5 %collective-permute-done = bf16[6,12,128,128]{3,2,1,0:T(8,128)(2,1)S(1)} collective-permute-done((bf16[6,12,128,128]{3,2,1,0:T(8,128)(2,1)}, bf16[6,12,128,128]{3,2,1,0:T(8,128)(2,1)S(1)}, u32[]{:S(2)}, u32[]{:S(2)}) %collective-permute-start) | collective-permute-done | bytes 2359328 | tf_op jit(solution)/shard_map/ppermute | solution.py:17
  265.3 26.9 %collective-permute-done.1 = bf16[6,12,128,128]{3,2,1,0:T(8,128)(2,1)} collective-permute-done((bf16[6,12,128,128]{3,2,1,0:T(8,128)(2,1)}, bf16[6,12,128,128]{3,2,1,0:T(8,128)(2,1)}, u32[]{:S(2)}, u32[]{:S(2)}) %collective-permute-start.1) | collective-permute-done | bytes 2359328 | tf_op jit(solution)/shard_map/ppermute | solution.py:18
  292.2 13.8 %pad_maximum_fusion = bf16[44,12,128,128]{3,2,1,0:T(8,128)(2,1)} fusion(bf16[6,12,128,128]{3,2,1,0:T(8,128)(2,1)} %collective-permute-done.1, bf16[32,12,128,128]{3,2,1,0:T(8,128)(2,1)} %all-gather.2.cloned.1.call-done, bf16[6,12,128,128]{3,2,1,0:T(8,128)(2,1)S(1)} %collective-permute-done), kind=kLoop, calls=%fused_computation.30 | loop fusion | flops 17301504 | bytes 34603008 | tf_op jit(solution)/shard_map/concatenate | solution.py:19
  306.0 851.9 %while.12 = (s32[]{:T(128)}, bf16[32,25,32,128]{3,2,1,0:T(8,128)(2,1)}, s32[32,25,32,128]{3,2,1,0:T(8,128)}, s32[32,12]{1,0:T(8,128)S(1)}, s32[32]{0:T(128)S(1)}...) while((s32[]{:T(128)}, ...), condition=%wide.region_3.4_spmd, body=%wide.region_0.3_spmd.sunk | while | flops 153201616 | bytes 25959816 | solution.py:86
  310.4 9.4 gather_fusion.1
  323.2 6.4 scatter_fusion
  337.0 9.4 gather_fusion.1
  349.8 6.4 scatter_fusion
  363.6 9.4 gather_fusion.1
  376.4 6.4 scatter_fusion
  390.2 9.4 gather_fusion.1
  403.0 6.4 scatter_fusion
  416.8 9.4 gather_fusion.1
  429.7 6.4 scatter_fusion
  443.5 9.4 gather_fusion.1
  456.3 6.4 scatter_fusion
  470.1 9.4 gather_fusion.1
  482.9 6.4 scatter_fusion
  496.7 9.4 gather_fusion.1
  509.5 6.4 scatter_fusion
  523.3 9.4 gather_fusion.1
  536.2 6.4 scatter_fusion
  550.0 9.4 gather_fusion.1
  562.8 6.4 scatter_fusion
  576.6 9.4 gather_fusion.1
  589.4 6.4 scatter_fusion
  603.2 9.4 gather_fusion.1
  629.8 9.4 gather_fusion.1
  642.6 6.4 scatter_fusion
  656.4 9.4 gather_fusion.1
  683.1 9.4 gather_fusion.1
  695.9 6.4 scatter_fusion
  709.7 9.4 gather_fusion.1
  722.5 6.4 scatter_fusion
  736.3 9.4 gather_fusion.1
  749.1 6.4 scatter_fusion
  762.9 9.4 gather_fusion.1
  775.8 6.4 scatter_fusion
  789.6 9.4 gather_fusion.1
  802.4 6.4 scatter_fusion
  816.2 9.4 gather_fusion.1
  829.0 6.4 scatter_fusion
  842.8 9.4 gather_fusion.1
  855.6 6.4 scatter_fusion
  869.4 9.4 gather_fusion.1
  896.1 9.4 gather_fusion.1
  922.7 9.4 gather_fusion.1
  935.5 6.4 scatter_fusion
  949.3 9.4 gather_fusion.1
  962.1 6.4 scatter_fusion
  975.9 9.4 gather_fusion.1
  988.7 6.4 scatter_fusion
  1002.5 9.4 gather_fusion.1
  1015.4 6.4 scatter_fusion
  1029.2 9.4 gather_fusion.1
  1042.0 6.4 scatter_fusion
  1055.8 9.4 gather_fusion.1
  1068.6 6.4 scatter_fusion
  1082.4 9.4 gather_fusion.1
  1109.0 9.4 gather_fusion.1
  1121.9 6.4 scatter_fusion
  1135.6 9.4 gather_fusion.1
  1148.5 6.4 scatter_fusion
  (569 shorter events, 353.6 us)
Async XLA Ops:
  6.5 222.8 %all-gather.2.cloned.1.call-start = ((), (), s32[]{:S(2)}) async-start(), calls=%async_computation | async-start | bytes 15728640 | tf_op jit(solution)/shard_map/all_gather | solution.py:63
  7.3 233.9 %copy-start = (s32[256,12]{0,1:T(8,128)S(1)}, s32[256,12]{0,1:T(8,128)}, u32[]{:S(2)}) copy-start(s32[256,12]{0,1:T(8,128)} %param.7) | copy-start | bytes 36868
  7.3 234.1 %copy-start.1 = (s32[256]{0:T(256)S(1)}, s32[256]{0:T(256)}, u32[]{:S(2)}) copy-start(s32[256]{0:T(256)} %param.8) | copy-start | bytes 3076
  235.7 29.6 %collective-permute-start = (bf16[6,12,128,128]{3,2,1,0:T(8,128)(2,1)}, bf16[6,12,128,128]{3,2,1,0:T(8,128)(2,1)S(1)}, u32[]{:S(2)}, u32[]{:S(2)}) collective-permute-start(bf16[6,12,128,128]{3,2,1,0:T(8,128)(2,1)} %get-tuple-element.181), channel_id=1, source_target_pairs={{0,1},{1,2},{2,3},{3,4},{4,5},{5,6},{6,7},{8,9},{9,10},{10,11},{11... | collective-permute-start | bytes 7077896 | tf_op jit(solution)/shard_map/ppermute | solution.py:17
  239.2 53.0 %collective-permute-start.1 = (bf16[6,12,128,128]{3,2,1,0:T(8,128)(2,1)}, bf16[6,12,128,128]{3,2,1,0:T(8,128)(2,1)}, u32[]{:S(2)}, u32[]{:S(2)}) collective-permute-start(bf16[6,12,128,128]{3,2,1,0:T(8,128)(2,1)} %get-tuple-element.182), channel_id=1, source_target_pairs={{1,0},{2,1},{3,2},{4,3},{5,4},{6,5},{7,6},{9,8},{10,9},{11,10},{12... | collective-permute-start | bytes 7077896 | tf_op jit(solution)/shard_map/ppermute | solution.py:18
Sparse Core Ops, SparseCore 0:
  8.9 220.4 all-gather.1
where the time goes:
time: 1170 us; the launch traced here: 1160 us
  local copies, waits for them, and re-layouts  391 us (33%)
  other arithmetic  342 us (29%)
  waiting for transfers between devices  273 us (23%)
  matrix products  100 us (9%)
  loops' own time  38.6 us (3%)
  between operations  13.5 us (1%)
    gather x32, local copies, waits for them, and re-layouts, expand(): firsts = banded[where_at]  300 us
    all_gather x1, waiting for transfers between devices, shards(): whole_cols = lax.all_gather(tiles, 'section', axis=2, tiled=True)  222 us
    scatter-add x32, other arithmetic, expand(): empty.at[target.reshape(-1)]  205 us
    dot_general x32, matrix products, expand(): jnp.einsum('kcx,klxr->klcr', own, firsts, preferred_element_type=jnp.floa...  100 us
    dynamic_update_slice x32, other arithmetic, shards(): lax.map(one_panel, (tiles, own_off, own_cnt, ranks, jnp.arange(panels, dt...  57.9 us
    dynamic_slice x64, local copies, waits for them, and re-layouts, shards(): lax.map(one_panel, (tiles, own_off, own_cnt, ranks, jnp.arange(panels, dt...  39.3 us
    another operation x1, loops' own time, shards(): lax.map(one_panel, (tiles, own_off, own_cnt, ranks, jnp.arange(panels, dt...  38.6 us
    reduce_sum x32, other arithmetic, finish(): totals = jnp.sum(squared, axis=(0, 2), keepdims=True)  37.7 us
  transfers between devices with their start and end apart: 3, of which 3 were waited for; matrix products, arithmetic and copies ran while one was open for 0% of the time, Pallas kernels for 0%

commit v1 on v0

v1 whole, which is shorter than its diff:
```python
import functools

import jax
import jax.numpy as jnp
from jax import lax
from jax.experimental import pallas as pl
from jax.experimental.pallas import tpu as pltpu
from jax.sharding import PartitionSpec as P

W = 6
TOPK = 256
HALF = 6


def panel_kernel(
    bands, slots, parts, panel_of,
    own_start, own_count, own_off, band_start, band_count, band_off,
    *refs,
):
    n_parts = len(parts)
    sources = refs[:n_parts]
    own_ref, ranks_ref = refs[n_parts], refs[n_parts + 1]
    out_ref, band, acc, sems = refs[-4:]
    step = pl.program_id(0)

    @pl.when(step == 0)
    def _():
        copies = [
            pltpu.make_async_copy(src, band.at[pl.ds(at, src.shape[0])], sems.at[i])
            for i, (src, at) in enumerate(zip(sources, parts))
        ]
        for copy in copies:
            copy.start()
        for copy in copies:
            copy.wait()

    panel = panel_of(step)
    acc[...] = jnp.zeros_like(acc)
    first = own_start[panel]

    def one_slot(q, carry):
        off = own_off[q]
        source = panel + W + off
        start = band_start[source]
        count = band_count[source]
        lhs = own_ref[q]

        def group(base):
            for i in range(base, min(base + HALF, slots)):
                product = jnp.dot(lhs, band[start + i], preferred_element_type=jnp.float32)
                where = jnp.where(i < count, off + band_off[start + i] + 2 * W, bands)
                acc[where] += product

        group(0)
        for base in range(HALF, slots, HALF):
            pl.when(count > base)(functools.partial(group, base))
        return carry

    lax.fori_loop(first, first + own_count[panel], one_slot, 0)

    total = jnp.zeros(acc.shape[1:], jnp.float32)
    for o in range(bands):
        value = acc[o]
        squared = jnp.where(ranks_ref[0, o] < TOPK, value * value, 0.0)
        acc[o] = squared
        total = total + squared
    totals = jnp.sum(total, axis=1, keepdims=True) + 1e-06
    scale = jnp.broadcast_to(TOPK / totals, total.shape)
    for o in range(bands):
        out_ref[0, o] = (acc[o] * scale).astype(out_ref.dtype)


def run_panels(scalars, sources, parts, size, own, ranks, steps, panel_of, previous):
    panels, bands, columns, rows = ranks.shape
    slots = scalars[-1]
    tables = scalars[:-1]
    block = (1, bands, columns, rows)
    panel_block = pl.BlockSpec(block, lambda i, *_: (panel_of(i), 0, 0, 0))
    operands = [*sources, own, ranks]
    specs = [pl.BlockSpec(memory_space=pl.ANY)] * len(sources)
    specs += [pl.BlockSpec(own.shape, lambda i, *_: (0, 0, 0)), panel_block]
    aliases = {}
    if previous is not None:
        aliases = {len(tables) + len(operands): 0}
        operands.append(previous)
        specs.append(pl.BlockSpec(memory_space=pl.ANY))
    return pl.pallas_call(
        functools.partial(panel_kernel, bands, slots, parts, panel_of),
        grid_spec=pltpu.PrefetchScalarGridSpec(
            num_scalar_prefetch=len(tables),
            grid=(steps,),
            in_specs=specs,
            out_specs=panel_block,
            scratch_shapes=[
                pltpu.VMEM((size, rows, rows), jnp.bfloat16),
                pltpu.VMEM((bands + 1, columns, rows), jnp.float32),
                pltpu.SemaphoreType.DMA((len(sources),)),
            ],
        ),
        out_shape=jax.ShapeDtypeStruct(ranks.shape, jnp.bfloat16),
        input_output_aliases=aliases,
        compiler_params=pltpu.CompilerParams(
            dimension_semantics=("arbitrary",), vmem_limit_bytes=56 * 2**20
        ),
        cost_estimate=pl.CostEstimate(
            flops=steps * 40 * 10**6, bytes_accessed=steps * 2 * 10**6, transcendentals=0
        ),
    )(*tables, *operands)


def shards(tiles, offsets, counts, ranks):
    panels, slots, columns, rows = tiles.shape
    total = offsets.shape[0]
    groups = lax.axis_size("col")
    me = lax.axis_index("col")
    full = panels * slots
    halo = W * slots

    slot_ids = jnp.arange(slots, dtype=jnp.int32)[None]
    row_of = jnp.arange(total, dtype=jnp.int32)[:, None] + offsets
    valid = (slot_ids < counts[:, None]) & (row_of >= 0) & (row_of < total)
    valid = valid.reshape(groups, full)
    needed = jnp.max(jnp.sum(valid.astype(jnp.int32), axis=1))

    def three(array):
        padded = jnp.pad(array, ((1, 1), (0, 0)))
        return lax.dynamic_slice_in_dim(padded, me, 3, 0)

    near_valid = three(valid.astype(jnp.int32))
    near_off = three(offsets.reshape(groups, full))
    ids = jnp.arange(full, dtype=jnp.int32)
    position = jnp.sum(
        jnp.where(ids[None, None, :] < ids[None, :, None], near_valid[:, None, :], 0), axis=2
    )
    packed = jnp.where(near_valid > 0, position, -1)
    match = packed[:, None, :] == ids[None, :, None]
    packed_off = jnp.sum(jnp.where(match, near_off[:, None, :], 0), axis=2)
    packed_id = jnp.sum(jnp.where(match[1], ids[None, :], 0), axis=1)
    panel_start = position.reshape(3, panels, slots)[:, :, 0]
    panel_count = jnp.sum(near_valid.reshape(3, panels, slots), axis=2)
    last_start = jnp.sum(near_valid, axis=1) - halo

    flat = tiles.reshape(full, columns, rows)
    up = [(i, i + 1) for i in range(groups - 1)]
    down = [(i + 1, i) for i in range(groups - 1)]

    def at_capacity(capacity):
        def run():
            own = flat[packed_id[:capacity]]
            gathered = lax.all_gather(own, "section", axis=1, tiled=True)
            starts = jnp.clip(last_start, 0, capacity - halo)
            last = lax.dynamic_slice_in_dim(gathered, starts[1], halo, 0)
            before = lax.ppermute(last, "col", up)
            after = lax.ppermute(gathered[:halo], "col", down)

            band_start = jnp.concatenate([
                panel_start[0, panels - W:] - starts[0],
                panel_start[1] + halo,
                panel_start[2, :W] + halo + capacity,
            ])
            band_count = jnp.concatenate(
                [panel_count[0, panels - W:], panel_count[1], panel_count[2, :W]]
            )
            band_off = jnp.concatenate([
                lax.dynamic_slice_in_dim(packed_off[0], starts[0], halo, 0),
                packed_off[1, :capacity],
                packed_off[2, :halo],
                jnp.zeros((slots,), jnp.int32),
            ])
            scalars = (
                panel_start[1], panel_count[1], packed_off[1],
                band_start, band_count, band_off, slots,
            )
            size = capacity + 2 * halo + slots
            inner = run_panels(
                scalars, [gathered], [halo], size, own, ranks,
                panels - 2 * W, lambda i: i + W, None,
            )
            return run_panels(
                scalars, [before, gathered, after], [0, halo, halo + capacity], size, own, ranks,
                2 * W, lambda i: jnp.where(i < W, i, i + panels - 2 * W), inner,
            )
        return run

    levels = sorted({max(halo, full * part // 24) for part in (14, 15, 16, 18, 24)})
    which = sum((needed > level).astype(jnp.int32) for level in levels[:-1])
    return lax.switch(which, [at_capacity(level) for level in levels])


def solution(mesh):
    placed = (P("col", None, "section", None), P(), P(), P("col", None, "section", None))
    return jax.shard_map(
        shards,
        mesh=mesh,
        in_specs=placed,
        out_specs=P("col", None, "section", None),
        check_vma=False,
    )
```

time: 1170 us -> 263 us (0.22)
  local copies, waits for them, and re-layouts: 391 us -> 16.2 us
  other arithmetic: 342 us -> 6.06 us
  waiting for transfers between devices: 273 us -> 141 us
  matrix products: 100 us -> 0 us
  Pallas kernels: 0 us -> 76.6 us
  loops' own time: 38.6 us -> 4.11 us
    gather x96 -> x1, local copies, waits for them, and re-layouts: 339 us -> 4.04 us  [run(): own = flat[packed_id[:capacity]]]
    scatter-add x32 -> x0, other arithmetic: 205 us -> none  [expand(): empty.at[target.reshape(-1)]]
    dot_general x32 -> x0, matrix products: 100 us -> none  [expand(): jnp.einsum('kcx,klxr->klcr', own, firsts, preferred_element_type=jnp.floa...]
    all_gather x1, waiting for transfers between devices: 222 us -> 141 us  [run(): gathered = lax.all_gather(own, 'section', axis=1, tiled=True)]
    pallas_call x0 -> x2, Pallas kernels: none -> 76.6 us  [run_panels(): pl.pallas_call(functools.partial(panel_kernel, bands, slots, parts, panel...]
    dynamic_update_slice x32 -> x0, other arithmetic: 57.9 us -> none  [shards(): lax.map(one_panel, (tiles, own_off, own_cnt, ranks, jnp.arange(panels, dt...]
    ppermute x2, waiting for transfers between devices: 50.4 us -> 0.01 us  [the longest x1 0.01 us: run(): before = lax.ppermute(last, 'col', up)]
    dynamic_slice x67 -> x1, local copies, waits for them, and re-layouts: 39.6 us -> 0.07 us  [run(): lax.dynamic_slice_in_dim(packed_off[0], starts[0], halo, 0)]
  transfers between devices with their start and end apart: 3 -> 3, of which waited for: 3 -> 1; matrix products, arithmetic and copies ran while one was open for 0% -> 2% of each run, Pallas kernels for 0% -> 18%
where the time goes in v1:
time: 263 us; the launch traced here: 265 us
  waiting for transfers between devices  141 us (54%)
  Pallas kernels  76.6 us (29%)
  local copies, waits for them, and re-layouts  16.2 us (6%)
  between operations  16 us (6%)
  other arithmetic  6.06 us (2%)
  starting transfers between devices  5.59 us (2%)
  loops' own time  4.11 us (2%)
    all_gather x1, waiting for transfers between devices, run(): gathered = lax.all_gather(own, 'section', axis=1, tiled=True)  141 us
    pallas_call x2, Pallas kernels, run_panels(): pl.pallas_call(functools.partial(panel_kernel, bands, slots, parts, panel...  76.6 us
    slice x1, local copies, waits for them, and re-layouts, run(): after = lax.ppermute(gathered[:halo], 'col', down)  5.64 us
  transfers between devices with their start and end apart: 3, of which 1 were waited for; matrix products, arithmetic and copies ran while one was open for 2% of the time, Pallas kernels for 18%

profile of v1, /device:TPU:1, one launch (start us, length us, event | category | flops | bytes accessed | tf_op | source)
XLA Modules:
  0.0 265.1 jit_solution(1470524567741362457)
XLA Ops:
  6.5 0.7 convert_reduce_fusion
  7.3 0.1 reduce_sum.62
  7.4 0.1 reduce_sum.63
  7.5 0.6 reduce_max.9
  10.7 0.1 copy.53
  10.9 0.1 convert_element_type.25
  11.1 0.3 select_reduce_fusion.10
  11.4 0.9 broadcast_in_dim.76
  12.3 0.1 eq.14
  12.4 0.1 broadcast_in_dim.73
  12.5 245.7 %conditional.1 = (bf16[32,25,32,128]{3,2,1,0:T(8,128)(2,1)}) conditional(s32[]{:T(128)} %clamp.8, (s32[3,384]{1,0:T(4,128)S(1)}, s32[3,384]{1,0:T(4,128)S(1)}, s32[3,384]{1,0:T(4,128)S(1)}, s32[3,384]{1,0:T(4,128)S(1)}, s32[3,384,384]{2,1,0:T(8,128)S(1)}, /*index=5*/bf16[32,12,32,128]{3,2,1,0:T(8,128)(2,1)}, ...), branch_computations={%region_8.9_spmd, %region_9.10_spmd, %region_10.11_spmd, %region_1... | conditional | flops 1281628928 | bytes 162477664 | solution.py:187
  12.5 0.0 all-gather.13.cloned.1.call-start
  12.6 1.5 copy.55
  14.1 1.6 reshape.80
  15.7 0.0 copy-start.1
  15.7 0.8 pad_dynamic-slice_fusion.1
  16.5 1.0 select_reduce_fusion.2
  17.5 0.0 copy-done.1
  17.5 0.2 select_reduce_fusion.3
  17.7 4.0 %gather_fusion.1 = bf16[240,32,128]{2,1,0:T(8,128)(2,1)} fusion(bf16[384,32,128]{2,1,0:T(8,128)(2,1)} %bitcast.109, s32[1024]{0:T(1024)S(1)} %pad_clamp_fusion.1), kind=kCustom, calls=%fused_computation.1 | custom fusion | bytes 3933120 | tf_op jit(solution)/shard_map/cond/branch_1_fun/gather | solution.py:149
  21.7 0.0 all-gather.13.cloned.1.call-update
  21.7 0.1 reduce_sum.85
  21.9 0.7 fusion.14
  24.6 0.0 copy-start.11
  24.6 140.6 %all-gather.13.cloned.1.call-done.refs_0_.refs_1_ = bf16[240,128,128]{2,1,0:T(8,128)(2,1)} async-done(((bf16[240,32,128]{2,1,0:T(8,128)(2,1)}), bf16[240,128,128]{2,1,0:T(8,128)(2,1)}) %all-gather.13.cloned.1.call-update) | async-done | bytes 7864336 | tf_op jit(solution)/shard_map/cond/branch_1_fun/all_gather | solution.py:150
  165.2 5.6 %fusion.12 = (bf16[72,128,128]{2,1,0:T(8,128)(2,1)}, bf16[72,128,128]{2,1,0:T(8,128)(2,1)S(1)}) fusion(bf16[240,128,128]{2,1,0:T(8,128)(2,1)} %all-gather.13.cloned.1.call-done.refs_0_.refs_1_, s32[]{:T(128)S(6)} %select_n.50), kind=kLoop, calls=%fused_computation.143 | loop fusion | bytes 9437188 | tf_op jit(solution)/shard_map/cond/branch_1_fun/slice | solution.py:154
  170.8 2.4 collective-permute-start.3
  173.2 3.1 %collective-permute-start.2 = (bf16[72,128,128]{2,1,0:T(8,128)(2,1)S(1)}, bf16[72,128,128]{2,1,0:T(8,128)(2,1)}, u32[]{:S(2)}, u32[]{:S(2)}) collective-permute-start(bf16[72,128,128]{2,1,0:T(8,128)(2,1)S(1)} %get-tuple-element.754), channel_id=1, source_target_pairs={{0,1},{1,2},{2,3},{3,4},{4,5},{5,6},{6,7},{8,9},{9,10},{10,11},{11... | collective-permute-start | bytes 7077896 | tf_op jit(solution)/shard_map/cond/branch_1_fun/ppermute | solution.py:153
  176.4 0.1 reshape.75
  177.6 0.1 reshape.70
  177.7 0.1 reduce_sum.70
  177.8 0.0 copy-done.11
  178.4 0.6 fusion.13
  179.0 0.1 fusion.1
  179.1 0.1 slice_reduce_fusion.4.own_start
  179.2 0.0 copy-start.19
  179.2 0.1 slice_reduce_fusion.3
  179.4 0.0 copy-start.22
  179.4 0.1 slice_bitcast_fusion.8
  179.5 0.6 subtract_bitcast_fusion.1
  180.1 0.6 pad_add_fusion.4
  180.7 0.7 pad_add_fusion.3.band_off
  181.4 0.0 copy-done.19
  181.4 0.0 copy-done.22
  181.4 46.7 %branch_1_fun.2.refs_5_ = bf16[32,25,32,128]{3,2,1,0:T(8,128)(2,1)} custom-call(s32[32]{0:T(128)} %copy-done.19, s32[32]{0:T(128)} %copy-done.22, s32[384]{0:T(512)} %get-tuple-element.756.own_off, s32[44]{0:T(128)} %get-tuple-element.765.band_start, s32[44]{0:T(128)} %get-tuple-element.766.band_count, s32[396]{0:T(512)} %pad_add_fusion.3.band_off, ...), custom_call_target="tpu_custom_call" | custom-call | flops 800000000 | bytes 40000000 | tf_op jit(solution)/shard_map/cond/branch_1_fun/pallas_call | solution.py:87
  228.1 0.0 collective-permute-done.3.refs_2_
  228.1 0.0 collective-permute-done.2.refs_0_
  228.1 29.9 %branch_1_fun.3 = bf16[32,25,32,128]{3,2,1,0:T(8,128)(2,1)} custom-call(s32[32]{0:T(128)} %copy-done.19, s32[32]{0:T(128)} %copy-done.22, s32[384]{0:T(512)} %get-tuple-element.756.own_off, s32[44]{0:T(128)} %get-tuple-element.765.band_start, s32[44]{0:T(128)} %get-tuple-element.766.band_count, ...), custom_call_target="tpu_custom_call", output_to_operand_aliasing={{}: (11, {})} | custom-call | flops 480000000 | bytes 24000000 | tf_op jit(solution)/shard_map/cond/branch_1_fun/pallas_call | solution.py:87
  (10 shorter events, 0.1 us)
Async XLA Ops:
  12.5 152.6 %all-gather.13.cloned.1.call-start = ((), (), s32[]{:S(2)}) async-start(), calls=%async_computation.1 | async-start | bytes 9830400 | tf_op jit(solution)/shard_map/cond/branch_1_fun/all_gather | solution.py:150
  15.7 1.8 copy-start.1
  24.6 153.2 %copy-start.11 = (s32[3,384]{1,0:T(4,128)S(1)}, s32[3,384]{1,0:T(4,128)}, u32[]{:S(2)}) copy-start(s32[3,384]{1,0:T(4,128)} %get-tuple-element.729) | copy-start | bytes 13828 | tf_op jit(solution)/shard_map/cond
  170.8 57.3 %collective-permute-start.3 = (bf16[72,128,128]{2,1,0:T(8,128)(2,1)}, bf16[72,128,128]{2,1,0:T(8,128)(2,1)}, u32[]{:S(2)}, u32[]{:S(2)}) collective-permute-start(bf16[72,128,128]{2,1,0:T(8,128)(2,1)} %get-tuple-element.753), channel_id=1, source_target_pairs={{1,0},{2,1},{3,2},{4,3},{5,4},{6,5},{7,6},{9,8},{10,9},{11,10},{12... | collective-permute-start | bytes 7077896 | tf_op jit(solution)/shard_map/cond/branch_1_fun/ppermute | solution.py:154
  173.2 54.9 %collective-permute-start.2 = (bf16[72,128,128]{2,1,0:T(8,128)(2,1)S(1)}, bf16[72,128,128]{2,1,0:T(8,128)(2,1)}, u32[]{:S(2)}, u32[]{:S(2)}) collective-permute-start(bf16[72,128,128]{2,1,0:T(8,128)(2,1)S(1)} %get-tuple-element.754), channel_id=1, source_target_pairs={{0,1},{1,2},{2,3},{3,4},{4,5},{5,6},{6,7},{8,9},{9,10},{10,11},{11... | collective-permute-start | bytes 7077896 | tf_op jit(solution)/shard_map/cond/branch_1_fun/ppermute | solution.py:153
  179.2 2.2 copy-start.19
  179.4 2.0 copy-start.22
Sparse Core Ops, SparseCore 0:
  21.9 143.2 all-gather.12
